TPU v7x, 32 devices: a whole 2x2x4 slice. The times are simulated.
32 devices in a mesh: region: 4 (over y, x), blk: 8 (over z, core).
Axes of the slice: x: 2, y: 2, z: 4, core: 2. Of those that a mesh axis runs over, the one named last changes fastest.
Arguments:
- incident: bfloat16 [8, 4, 64, 32, 128], P(None, 'region', 'blk'), may hold values from -6 to 6
- past_currents: bfloat16 [4, 4, 64, 32, 128], P(None, 'region', 'blk'), may hold values from -6 to 6
- self_inverse: bfloat16 [4, 64, 128, 128], P('region', 'blk'), may hold values from -0.5 to 0.5
- near_tiles: bfloat16 [4, 64, 32, 128, 128], P('region', 'blk'), may hold values from -0.046875 to 0.046875
- near_cols: int32 [4, 64, 32], P('region', 'blk'), may hold values from 0 to 63, as said below
- near_delay: int32 [4, 64, 32], P('region', 'blk'), may hold values from 1 to 4
- block_slot: int32 [4, 64], P('region'), may hold values from 0 to 63, as said below
- far_out: bfloat16 [4, 64, 128, 64], P('region', 'blk'), may hold values from -0.03125 to 0.03125
- far_in: bfloat16 [4, 64, 64, 128], P('region', 'blk'), may hold values from -0.75 to 0.75
- far_pairs: int32 [4, 3], P('region'), may hold values from 0 to 3, as said below
- far_delay: int32 [4, 3], P('region'), may hold values from 1 to 4
- far_coupling: float32 [4, 3, 64, 64], P('region'), may hold values from -0.4375 to 0.4375
Outputs:
- currents: bfloat16 [8, 4, 64, 32, 128], P(None, 'region', 'blk')
Inputs may be any that keep to these rules, and one draw needn't show every extreme that they name: `block_slot`: each region's ids are a permutation of 0 to 63. `near_cols`: for block row at position b, every near source block is stored on a blk device at most 4 devices from the device of b, and the first tile of every row lies exactly 4 devices away. `far_pairs`: region g lists each of the other 3 regions exactly once.
All inputs are finite; a program needn't handle non-finite values.
Results may differ from a plain program's by a relative error of at most 0.01.
Values may be sent and summed in bfloat16 or wider, within the bound.
A program may use at most 64 MiB of HBM per device.

v0:
```python
import jax
import jax.numpy as jnp
from jax import lax
from jax.sharding import PartitionSpec as P

REACH = 4


def shifted(value, axis, by):
    devices = lax.axis_size(axis)
    pairs = [(i, i + by) for i in range(devices) if 0 <= i + by < devices]
    return lax.ppermute(value, axis, pairs)


def reach_window(blocks, dim):
    lower = []
    upper = []
    below = blocks
    above = blocks
    for stride in range(REACH):
        below = shifted(below, "blk", 1)
        above = shifted(above, "blk", -1)
        lower.append(below)
        upper.append(above)
    pieces = lower[::-1] + [blocks] + upper
    return jnp.concatenate(pieces, axis=dim)


def on_device(
    incident,
    past_currents,
    self_inverse,
    near_tiles,
    near_cols,
    near_delay,
    block_slot,
    far_out,
    far_in,
    far_pairs,
    far_delay,
    far_coupling,
):
    per_device = near_cols.shape[1]
    device = lax.axis_index("blk")
    position = block_slot[0][near_cols[0]]
    delay_index = near_delay[0] - 1
    local_pos = position - (device - REACH) * per_device

    def project(stacked):
        partial_value = jnp.einsum(
            "nbpr,brk->npk", stacked, far_out[0], preferred_element_type=jnp.float32
        )
        summed = lax.psum(partial_value, "blk")
        result = lax.all_gather(summed[:, None], "region", axis=1, tiled=True)
        return result

    history = reach_window(past_currents[:, 0], 1)
    moment_hist = project(past_currents[:, 0])

    def advance(history, moment_hist, incoming):
        sources = moment_hist[far_delay[0] - 1, far_pairs[0]]
        blended = jnp.einsum(
            "fpk,fkl->pl", sources, far_coupling[0], precision=lax.Precision.HIGHEST
        ).astype(jnp.bfloat16)
        far_field = jnp.einsum(
            "pk,bkr->bpr", blended, far_in[0], preferred_element_type=jnp.float32
        )
        gathered = history[delay_index, local_pos]
        near_field = jnp.einsum(
            "bjpk,bjkm->bpm", gathered, near_tiles[0], preferred_element_type=jnp.float32
        )
        driven = (incoming.astype(jnp.float32) - near_field - far_field).astype(jnp.bfloat16)
        return jnp.einsum(
            "bpk,bkm->bpm", driven, self_inverse[0], preferred_element_type=jnp.float32
        ).astype(jnp.bfloat16)

    def march(carry, incoming):
        history, moment_hist = carry
        current = advance(history, moment_hist, incoming)
        arrived = reach_window(current, 0)
        history = jnp.concatenate([arrived[None], history[:-1]], axis=0)
        moment_hist = jnp.concatenate([project(current[None]), moment_hist[:-1]], axis=0)
        return ((history, moment_hist), current)

    (history, moment_hist), earlier = lax.scan(march, (history, moment_hist), incident[:-1, 0])
    final = advance(history, moment_hist, incident[-1, 0])
    currents = jnp.concatenate([earlier, final[None]], axis=0)
    return currents[:, None]


def solution(mesh):
    in_specs = (
        P(None, "region", "blk", None, None),
        P(None, "region", "blk", None, None),
        P("region", "blk", None, None),
        P("region", "blk", None, None, None),
        P("region", "blk", None),
        P("region", "blk", None),
        P("region", None),
        P("region", "blk", None, None),
        P("region", "blk", None, None),
        P("region", None),
        P("region", None),
        P("region", None, None, None),
    )
    out_specs = P(None, "region", "blk", None, None)
    return jax.shard_map(
        on_device, mesh=mesh, in_specs=in_specs, out_specs=out_specs, check_vma=False
    )
```

profile of v0, /device:TPU:1, one launch (start us, length us, event | category | flops | bytes accessed | tf_op | source)
XLA Modules:
  0.0 569.0 jit_solution(6889944046948966961)
XLA Ops:
  0.0 4.7 collective-permute-start.8
  9.4 3.6 collective-permute-start.9
  16.3 4.4 collective-permute-start.10
  20.9 22.7 %psum.20 = f32[4,1,32,64]{3,2,0,1:T(8,128)S(1)} all-reduce(f32[4,1,32,64]{3,2,0,1:T(8,128)S(1)} %convolution_bitcast_fusion.4), channel_id=1, replica_groups=mesh['region'=4,'blk'=8] {'blk'}, use_global_device_ids=true, to_apply=%region_0.0 | all-reduce | flops 8192 | bytes 65536 | tf_op jit(solution)/shard_map/psum | solution.py:53
  43.7 6.1 %collective-permute-start.14 = (bf16[4,8,32,128]{3,2,1,0:T(8,128)(2,1)S(1)}, bf16[4,8,32,128]{3,2,1,0:T(8,128)(2,1)S(1)}, u32[]{:S(2)}, u32[]{:S(2)}) collective-permute-start(bf16[4,8,32,128]{3,2,1,0:T(8,128)(2,1)S(1)} %collective-permute-done.13), channel_id=1, source_target_pairs={{1,0},{2,1},{3,2},{4,3},{5,4},{6,5},{7,6},{9,8},{10,9},{11,10},{12... | collective-permute-start | bytes 786440 | tf_op jit(solution)/shard_map/ppermute | solution.py:12
  51.7 7.0 %all_gather.12 = f32[4,4,32,64]{3,2,0,1:T(8,128)S(1)} all-gather(f32[4,1,32,64]{3,2,0,1:T(8,128)S(1)} %psum.20), channel_id=1, replica_groups=mesh['region'=4,'blk'=8] {'region'}, dimensions={1}, use_global_device_ids=true | all-gather | bytes 163840 | tf_op jit(solution)/shard_map/all_gather | solution.py:54
  59.6 4.6 collective-permute-start.15
  68.9 490.1 %while.18 = (s32[]{:T(128)}, bf16[4,72,32,128]{3,2,1,0:T(8,128)(2,1)}, f32[4,4,32,64]{3,2,1,0:T(8,128)S(1)}, bf16[7,8,32,128]{3,2,1,0:T(8,128)(2,1)}, bf16[7,8,3...) while((s32[]{:T(128)}, ...), condition=%wide.region_3.4_spmd, body=%wide.region_1.3_spmd.sunk | while | flops 291314464 | bytes 27926540 | solution.py:85
  72.9 4.8 fusion.86
  83.0 3.2 collective-permute-start.1
  88.1 3.6 collective-permute-start.2
  93.8 22.2 %psum.22 = f32[1,1,32,64]{3,2,1,0:T(8,128)S(1)} all-reduce(f32[1,1,32,64]{3,2,1,0:T(8,128)S(1)} %convolution_bitcast_fusion.7), channel_id=1, replica_groups=mesh['region'=4,'blk'=8] {'blk'}, use_global_device_ids=true, to_apply=%region_2.2 | all-reduce | flops 2048 | bytes 16384 | tf_op jit(solution)/shard_map/while/body/eval_jaxpr/psum | solution.py:53
  115.9 6.2 %all_gather.14 = f32[1,4,32,64]{3,2,0,1:T(8,128)S(1)} all-gather(f32[1,1,32,64]{3,2,0,1:T(8,128)S(1)} %bitcast.240), channel_id=1, replica_groups=mesh['region'=4,'blk'=8] {'region'}, dimensions={1}, use_global_device_ids=true | all-gather | bytes 40960 | tf_op jit(solution)/shard_map/while/body/eval_jaxpr/all_gather | solution.py:54
  122.1 8.0 %collective-permute-start.6 = (bf16[8,32,128]{2,1,0:T(8,128)(2,1)S(1)}, bf16[8,32,128]{2,1,0:T(8,128)(2,1)S(1)}, u32[]{:S(2)}, u32[]{:S(2)}) collective-permute-start(bf16[8,32,128]{2,1,0:T(8,128)(2,1)S(1)} %collective-permute-done.5), channel_id=1, source_target_pairs={{1,0},{2,1},{3,2},{4,3},{5,4},{6,5},{7,6},{9,8},{10,9},{11,10},{12... | collective-permute-start | bytes 196616 | tf_op jit(solution)/shard_map/while/body/eval_jaxpr/ppermute | solution.py:12
  143.3 4.8 fusion.86
  158.6 3.6 collective-permute-start.2
  164.2 22.2 %psum.22 = f32[1,1,32,64]{3,2,1,0:T(8,128)S(1)} all-reduce(f32[1,1,32,64]{3,2,1,0:T(8,128)S(1)} %convolution_bitcast_fusion.7), channel_id=1, replica_groups=mesh['region'=4,'blk'=8] {'blk'}, use_global_device_ids=true, to_apply=%region_2.2 | all-reduce | flops 2048 | bytes 16384 | tf_op jit(solution)/shard_map/while/body/eval_jaxpr/psum | solution.py:53
  186.4 5.2 all_gather.14
  191.6 8.0 %collective-permute-start.6 = (bf16[8,32,128]{2,1,0:T(8,128)(2,1)S(1)}, bf16[8,32,128]{2,1,0:T(8,128)(2,1)S(1)}, u32[]{:S(2)}, u32[]{:S(2)}) collective-permute-start(bf16[8,32,128]{2,1,0:T(8,128)(2,1)S(1)} %collective-permute-done.5), channel_id=1, source_target_pairs={{1,0},{2,1},{3,2},{4,3},{5,4},{6,5},{7,6},{9,8},{10,9},{11,10},{12... | collective-permute-start | bytes 196616 | tf_op jit(solution)/shard_map/while/body/eval_jaxpr/ppermute | solution.py:12
  212.8 4.8 fusion.86
  222.9 3.2 collective-permute-start.1
  228.0 3.6 collective-permute-start.2
  233.7 22.2 %psum.22 = f32[1,1,32,64]{3,2,1,0:T(8,128)S(1)} all-reduce(f32[1,1,32,64]{3,2,1,0:T(8,128)S(1)} %convolution_bitcast_fusion.7), channel_id=1, replica_groups=mesh['region'=4,'blk'=8] {'blk'}, use_global_device_ids=true, to_apply=%region_2.2 | all-reduce | flops 2048 | bytes 16384 | tf_op jit(solution)/shard_map/while/body/eval_jaxpr/psum | solution.py:53
  255.8 6.2 %all_gather.14 = f32[1,4,32,64]{3,2,0,1:T(8,128)S(1)} all-gather(f32[1,1,32,64]{3,2,0,1:T(8,128)S(1)} %bitcast.240), channel_id=1, replica_groups=mesh['region'=4,'blk'=8] {'region'}, dimensions={1}, use_global_device_ids=true | all-gather | bytes 40960 | tf_op jit(solution)/shard_map/while/body/eval_jaxpr/all_gather | solution.py:54
  262.0 8.0 %collective-permute-start.6 = (bf16[8,32,128]{2,1,0:T(8,128)(2,1)S(1)}, bf16[8,32,128]{2,1,0:T(8,128)(2,1)S(1)}, u32[]{:S(2)}, u32[]{:S(2)}) collective-permute-start(bf16[8,32,128]{2,1,0:T(8,128)(2,1)S(1)} %collective-permute-done.5), channel_id=1, source_target_pairs={{1,0},{2,1},{3,2},{4,3},{5,4},{6,5},{7,6},{9,8},{10,9},{11,10},{12... | collective-permute-start | bytes 196616 | tf_op jit(solution)/shard_map/while/body/eval_jaxpr/ppermute | solution.py:12
  283.2 4.8 fusion.86
  293.3 3.2 collective-permute-start.1
  298.5 3.6 collective-permute-start.2
  304.1 22.2 %psum.22 = f32[1,1,32,64]{3,2,1,0:T(8,128)S(1)} all-reduce(f32[1,1,32,64]{3,2,1,0:T(8,128)S(1)} %convolution_bitcast_fusion.7), channel_id=1, replica_groups=mesh['region'=4,'blk'=8] {'blk'}, use_global_device_ids=true, to_apply=%region_2.2 | all-reduce | flops 2048 | bytes 16384 | tf_op jit(solution)/shard_map/while/body/eval_jaxpr/psum | solution.py:53
  326.3 5.2 all_gather.14
  331.5 8.0 %collective-permute-start.6 = (bf16[8,32,128]{2,1,0:T(8,128)(2,1)S(1)}, bf16[8,32,128]{2,1,0:T(8,128)(2,1)S(1)}, u32[]{:S(2)}, u32[]{:S(2)}) collective-permute-start(bf16[8,32,128]{2,1,0:T(8,128)(2,1)S(1)} %collective-permute-done.5), channel_id=1, source_target_pairs={{1,0},{2,1},{3,2},{4,3},{5,4},{6,5},{7,6},{9,8},{10,9},{11,10},{12... | collective-permute-start | bytes 196616 | tf_op jit(solution)/shard_map/while/body/eval_jaxpr/ppermute | solution.py:12
  352.7 4.8 fusion.86
  362.8 3.2 collective-permute-start.1
  367.9 3.6 collective-permute-start.2
  373.5 22.2 %psum.22 = f32[1,1,32,64]{3,2,1,0:T(8,128)S(1)} all-reduce(f32[1,1,32,64]{3,2,1,0:T(8,128)S(1)} %convolution_bitcast_fusion.7), channel_id=1, replica_groups=mesh['region'=4,'blk'=8] {'blk'}, use_global_device_ids=true, to_apply=%region_2.2 | all-reduce | flops 2048 | bytes 16384 | tf_op jit(solution)/shard_map/while/body/eval_jaxpr/psum | solution.py:53
  395.7 6.2 %all_gather.14 = f32[1,4,32,64]{3,2,0,1:T(8,128)S(1)} all-gather(f32[1,1,32,64]{3,2,0,1:T(8,128)S(1)} %bitcast.240), channel_id=1, replica_groups=mesh['region'=4,'blk'=8] {'region'}, dimensions={1}, use_global_device_ids=true | all-gather | bytes 40960 | tf_op jit(solution)/shard_map/while/body/eval_jaxpr/all_gather | solution.py:54
  401.9 8.0 %collective-permute-start.6 = (bf16[8,32,128]{2,1,0:T(8,128)(2,1)S(1)}, bf16[8,32,128]{2,1,0:T(8,128)(2,1)S(1)}, u32[]{:S(2)}, u32[]{:S(2)}) collective-permute-start(bf16[8,32,128]{2,1,0:T(8,128)(2,1)S(1)} %collective-permute-done.5), channel_id=1, source_target_pairs={{1,0},{2,1},{3,2},{4,3},{5,4},{6,5},{7,6},{9,8},{10,9},{11,10},{12... | collective-permute-start | bytes 196616 | tf_op jit(solution)/shard_map/while/body/eval_jaxpr/ppermute | solution.py:12
  423.1 4.8 fusion.86
  438.4 3.6 collective-permute-start.2
  444.0 22.2 %psum.22 = f32[1,1,32,64]{3,2,1,0:T(8,128)S(1)} all-reduce(f32[1,1,32,64]{3,2,1,0:T(8,128)S(1)} %convolution_bitcast_fusion.7), channel_id=1, replica_groups=mesh['region'=4,'blk'=8] {'blk'}, use_global_device_ids=true, to_apply=%region_2.2 | all-reduce | flops 2048 | bytes 16384 | tf_op jit(solution)/shard_map/while/body/eval_jaxpr/psum | solution.py:53
  466.2 5.2 all_gather.14
  471.4 8.0 %collective-permute-start.6 = (bf16[8,32,128]{2,1,0:T(8,128)(2,1)S(1)}, bf16[8,32,128]{2,1,0:T(8,128)(2,1)S(1)}, u32[]{:S(2)}, u32[]{:S(2)}) collective-permute-start(bf16[8,32,128]{2,1,0:T(8,128)(2,1)S(1)} %collective-permute-done.5), channel_id=1, source_target_pairs={{1,0},{2,1},{3,2},{4,3},{5,4},{6,5},{7,6},{9,8},{10,9},{11,10},{12... | collective-permute-start | bytes 196616 | tf_op jit(solution)/shard_map/while/body/eval_jaxpr/ppermute | solution.py:12
  492.6 4.8 fusion.86
  507.8 3.6 collective-permute-start.2
  513.4 22.2 %psum.22 = f32[1,1,32,64]{3,2,1,0:T(8,128)S(1)} all-reduce(f32[1,1,32,64]{3,2,1,0:T(8,128)S(1)} %convolution_bitcast_fusion.7), channel_id=1, replica_groups=mesh['region'=4,'blk'=8] {'blk'}, use_global_device_ids=true, to_apply=%region_2.2 | all-reduce | flops 2048 | bytes 16384 | tf_op jit(solution)/shard_map/while/body/eval_jaxpr/psum | solution.py:53
  535.6 6.2 %all_gather.14 = f32[1,4,32,64]{3,2,0,1:T(8,128)S(1)} all-gather(f32[1,1,32,64]{3,2,0,1:T(8,128)S(1)} %bitcast.240), channel_id=1, replica_groups=mesh['region'=4,'blk'=8] {'region'}, dimensions={1}, use_global_device_ids=true | all-gather | bytes 40960 | tf_op jit(solution)/shard_map/while/body/eval_jaxpr/all_gather | solution.py:54
  541.8 8.0 %collective-permute-start.6 = (bf16[8,32,128]{2,1,0:T(8,128)(2,1)S(1)}, bf16[8,32,128]{2,1,0:T(8,128)(2,1)S(1)}, u32[]{:S(2)}, u32[]{:S(2)}) collective-permute-start(bf16[8,32,128]{2,1,0:T(8,128)(2,1)S(1)} %collective-permute-done.5), channel_id=1, source_target_pairs={{1,0},{2,1},{3,2},{4,3},{5,4},{6,5},{7,6},{9,8},{10,9},{11,10},{12... | collective-permute-start | bytes 196616 | tf_op jit(solution)/shard_map/while/body/eval_jaxpr/ppermute | solution.py:12
  562.1 4.9 fusion.33
  (305 shorter events, 185.3 us)
Async XLA Ops:
  0.0 9.3 %collective-permute-start.8 = (bf16[4,8,32,128]{3,2,1,0:T(8,128)(2,1)}, bf16[4,8,32,128]{3,2,1,0:T(8,128)(2,1)S(1)}, u32[]{:S(2)}, u32[]{:S(2)}) collective-permute-start(bf16[4,8,32,128]{3,2,1,0:T(8,128)(2,1)} %bitcast.241), channel_id=1, source_target_pairs={{0,1},{1,2},{2,3},{3,4},{4,5},{5,6},{6,7},{8,9},{9,10},{10,11},{11... | collective-permute-start | bytes 786440 | tf_op jit(solution)/shard_map/ppermute | solution.py:12
  4.8 8.5 %collective-permute-start.12 = (bf16[4,8,32,128]{3,2,1,0:T(8,128)(2,1)}, bf16[4,8,32,128]{3,2,1,0:T(8,128)(2,1)S(1)}, u32[]{:S(2)}, u32[]{:S(2)}) collective-permute-start(bf16[4,8,32,128]{3,2,1,0:T(8,128)(2,1)} %bitcast.242), channel_id=1, source_target_pairs={{1,0},{2,1},{3,2},{4,3},{5,4},{6,5},{7,6},{9,8},{10,9},{11,10},{12... | collective-permute-start | bytes 786440 | tf_op jit(solution)/shard_map/ppermute | solution.py:12
  9.4 6.9 %collective-permute-start.9 = (bf16[4,8,32,128]{3,2,1,0:T(8,128)(2,1)S(1)}, bf16[4,8,32,128]{3,2,1,0:T(8,128)(2,1)S(1)}, u32[]{:S(2)}, u32[]{:S(2)}) collective-permute-start(bf16[4,8,32,128]{3,2,1,0:T(8,128)(2,1)S(1)} %collective-permute-done.8), channel_id=1, source_target_pairs={{0,1},{1,2},{2,3},{3,4},{4,5},{5,6},{6,7},{8,9},{9,10},{10,11},{11... | collective-permute-start | bytes 786440 | tf_op jit(solution)/shard_map/ppermute | solution.py:12
  13.3 30.4 %collective-permute-start.13 = (bf16[4,8,32,128]{3,2,1,0:T(8,128)(2,1)S(1)}, bf16[4,8,32,128]{3,2,1,0:T(8,128)(2,1)S(1)}, u32[]{:S(2)}, u32[]{:S(2)}) collective-permute-start(bf16[4,8,32,128]{3,2,1,0:T(8,128)(2,1)S(1)} %collective-permute-done.12), channel_id=1, source_target_pairs={{1,0},{2,1},{3,2},{4,3},{5,4},{6,5},{7,6},{9,8},{10,9},{11,10},{12... | collective-permute-start | bytes 786440 | tf_op jit(solution)/shard_map/ppermute | solution.py:12
  16.3 33.4 %collective-permute-start.10 = (bf16[4,8,32,128]{3,2,1,0:T(8,128)(2,1)S(1)}, bf16[4,8,32,128]{3,2,1,0:T(8,128)(2,1)S(1)}, u32[]{:S(2)}, u32[]{:S(2)}) collective-permute-start(bf16[4,8,32,128]{3,2,1,0:T(8,128)(2,1)S(1)} %collective-permute-done.9), channel_id=1, source_target_pairs={{0,1},{1,2},{2,3},{3,4},{4,5},{5,6},{6,7},{8,9},{9,10},{10,11},{11... | collective-permute-start | bytes 786440 | tf_op jit(solution)/shard_map/ppermute | solution.py:12
  43.7 15.9 %collective-permute-start.14 = (bf16[4,8,32,128]{3,2,1,0:T(8,128)(2,1)S(1)}, bf16[4,8,32,128]{3,2,1,0:T(8,128)(2,1)S(1)}, u32[]{:S(2)}, u32[]{:S(2)}) collective-permute-start(bf16[4,8,32,128]{3,2,1,0:T(8,128)(2,1)S(1)} %collective-permute-done.13), channel_id=1, source_target_pairs={{1,0},{2,1},{3,2},{4,3},{5,4},{6,5},{7,6},{9,8},{10,9},{11,10},{12... | collective-permute-start | bytes 786440 | tf_op jit(solution)/shard_map/ppermute | solution.py:12
  49.8 14.4 %collective-permute-start.11 = (bf16[4,8,32,128]{3,2,1,0:T(8,128)(2,1)S(1)}, bf16[4,8,32,128]{3,2,1,0:T(8,128)(2,1)S(1)}, u32[]{:S(2)}, u32[]{:S(2)}) collective-permute-start(bf16[4,8,32,128]{3,2,1,0:T(8,128)(2,1)S(1)} %collective-permute-done.10), channel_id=1, source_target_pairs={{0,1},{1,2},{2,3},{3,4},{4,5},{5,6},{6,7},{8,9},{9,10},{10,11},{11... | collective-permute-start | bytes 786440 | tf_op jit(solution)/shard_map/ppermute | solution.py:12
  59.6 7.8 %collective-permute-start.15 = (bf16[4,8,32,128]{3,2,1,0:T(8,128)(2,1)S(1)}, bf16[4,8,32,128]{3,2,1,0:T(8,128)(2,1)S(1)}, u32[]{:S(2)}, u32[]{:S(2)}) collective-permute-start(bf16[4,8,32,128]{3,2,1,0:T(8,128)(2,1)S(1)} %collective-permute-done.14), channel_id=1, source_target_pairs={{1,0},{2,1},{3,2},{4,3},{5,4},{6,5},{7,6},{9,8},{10,9},{11,10},{12... | collective-permute-start | bytes 786440 | tf_op jit(solution)/shard_map/ppermute | solution.py:12
  80.6 5.6 collective-permute-start.4
  83.0 5.1 collective-permute-start.1
  86.2 35.9 %collective-permute-start.5 = (bf16[8,32,128]{2,1,0:T(8,128)(2,1)S(1)}, bf16[8,32,128]{2,1,0:T(8,128)(2,1)S(1)}, u32[]{:S(2)}, u32[]{:S(2)}) collective-permute-start(bf16[8,32,128]{2,1,0:T(8,128)(2,1)S(1)} %collective-permute-done.4), channel_id=1, source_target_pairs={{1,0},{2,1},{3,2},{4,3},{5,4},{6,5},{7,6},{9,8},{10,9},{11,10},{12... | collective-permute-start | bytes 196616 | tf_op jit(solution)/shard_map/while/body/eval_jaxpr/ppermute | solution.py:12
  88.1 42.0 %collective-permute-start.2 = (bf16[8,32,128]{2,1,0:T(8,128)(2,1)S(1)}, bf16[8,32,128]{2,1,0:T(8,128)(2,1)S(1)}, u32[]{:S(2)}, u32[]{:S(2)}) collective-permute-start(bf16[8,32,128]{2,1,0:T(8,128)(2,1)S(1)} %collective-permute-done.1), channel_id=1, source_target_pairs={{0,1},{1,2},{2,3},{3,4},{4,5},{5,6},{6,7},{8,9},{9,10},{10,11},{11... | collective-permute-start | bytes 196616 | tf_op jit(solution)/shard_map/while/body/eval_jaxpr/ppermute | solution.py:12
  122.1 10.0 %collective-permute-start.6 = (bf16[8,32,128]{2,1,0:T(8,128)(2,1)S(1)}, bf16[8,32,128]{2,1,0:T(8,128)(2,1)S(1)}, u32[]{:S(2)}, u32[]{:S(2)}) collective-permute-start(bf16[8,32,128]{2,1,0:T(8,128)(2,1)S(1)} %collective-permute-done.5), channel_id=1, source_target_pairs={{1,0},{2,1},{3,2},{4,3},{5,4},{6,5},{7,6},{9,8},{10,9},{11,10},{12... | collective-permute-start | bytes 196616 | tf_op jit(solution)/shard_map/while/body/eval_jaxpr/ppermute | solution.py:12
  132.1 5.6 collective-permute-start.7
  151.0 5.6 collective-permute-start.4
  153.4 5.1 collective-permute-start.1
  156.6 35.0 %collective-permute-start.5 = (bf16[8,32,128]{2,1,0:T(8,128)(2,1)S(1)}, bf16[8,32,128]{2,1,0:T(8,128)(2,1)S(1)}, u32[]{:S(2)}, u32[]{:S(2)}) collective-permute-start(bf16[8,32,128]{2,1,0:T(8,128)(2,1)S(1)} %collective-permute-done.4), channel_id=1, source_target_pairs={{1,0},{2,1},{3,2},{4,3},{5,4},{6,5},{7,6},{9,8},{10,9},{11,10},{12... | collective-permute-start | bytes 196616 | tf_op jit(solution)/shard_map/while/body/eval_jaxpr/ppermute | solution.py:12
  158.6 41.1 %collective-permute-start.2 = (bf16[8,32,128]{2,1,0:T(8,128)(2,1)S(1)}, bf16[8,32,128]{2,1,0:T(8,128)(2,1)S(1)}, u32[]{:S(2)}, u32[]{:S(2)}) collective-permute-start(bf16[8,32,128]{2,1,0:T(8,128)(2,1)S(1)} %collective-permute-done.1), channel_id=1, source_target_pairs={{0,1},{1,2},{2,3},{3,4},{4,5},{5,6},{6,7},{8,9},{9,10},{10,11},{11... | collective-permute-start | bytes 196616 | tf_op jit(solution)/shard_map/while/body/eval_jaxpr/ppermute | solution.py:12
  191.6 10.0 %collective-permute-start.6 = (bf16[8,32,128]{2,1,0:T(8,128)(2,1)S(1)}, bf16[8,32,128]{2,1,0:T(8,128)(2,1)S(1)}, u32[]{:S(2)}, u32[]{:S(2)}) collective-permute-start(bf16[8,32,128]{2,1,0:T(8,128)(2,1)S(1)} %collective-permute-done.5), channel_id=1, source_target_pairs={{1,0},{2,1},{3,2},{4,3},{5,4},{6,5},{7,6},{9,8},{10,9},{11,10},{12... | collective-permute-start | bytes 196616 | tf_op jit(solution)/shard_map/while/body/eval_jaxpr/ppermute | solution.py:12
  201.6 5.6 collective-permute-start.7
  220.5 5.6 collective-permute-start.4
  222.9 5.1 collective-permute-start.1
  226.1 35.9 %collective-permute-start.5 = (bf16[8,32,128]{2,1,0:T(8,128)(2,1)S(1)}, bf16[8,32,128]{2,1,0:T(8,128)(2,1)S(1)}, u32[]{:S(2)}, u32[]{:S(2)}) collective-permute-start(bf16[8,32,128]{2,1,0:T(8,128)(2,1)S(1)} %collective-permute-done.4), channel_id=1, source_target_pairs={{1,0},{2,1},{3,2},{4,3},{5,4},{6,5},{7,6},{9,8},{10,9},{11,10},{12... | collective-permute-start | bytes 196616 | tf_op jit(solution)/shard_map/while/body/eval_jaxpr/ppermute | solution.py:12
  228.0 42.0 %collective-permute-start.2 = (bf16[8,32,128]{2,1,0:T(8,128)(2,1)S(1)}, bf16[8,32,128]{2,1,0:T(8,128)(2,1)S(1)}, u32[]{:S(2)}, u32[]{:S(2)}) collective-permute-start(bf16[8,32,128]{2,1,0:T(8,128)(2,1)S(1)} %collective-permute-done.1), channel_id=1, source_target_pairs={{0,1},{1,2},{2,3},{3,4},{4,5},{5,6},{6,7},{8,9},{9,10},{10,11},{11... | collective-permute-start | bytes 196616 | tf_op jit(solution)/shard_map/while/body/eval_jaxpr/ppermute | solution.py:12
  262.0 10.0 %collective-permute-start.6 = (bf16[8,32,128]{2,1,0:T(8,128)(2,1)S(1)}, bf16[8,32,128]{2,1,0:T(8,128)(2,1)S(1)}, u32[]{:S(2)}, u32[]{:S(2)}) collective-permute-start(bf16[8,32,128]{2,1,0:T(8,128)(2,1)S(1)} %collective-permute-done.5), channel_id=1, source_target_pairs={{1,0},{2,1},{3,2},{4,3},{5,4},{6,5},{7,6},{9,8},{10,9},{11,10},{12... | collective-permute-start | bytes 196616 | tf_op jit(solution)/shard_map/while/body/eval_jaxpr/ppermute | solution.py:12
  272.0 5.6 collective-permute-start.7
  290.9 5.6 collective-permute-start.4
  293.3 5.1 collective-permute-start.1
  296.5 35.0 %collective-permute-start.5 = (bf16[8,32,128]{2,1,0:T(8,128)(2,1)S(1)}, bf16[8,32,128]{2,1,0:T(8,128)(2,1)S(1)}, u32[]{:S(2)}, u32[]{:S(2)}) collective-permute-start(bf16[8,32,128]{2,1,0:T(8,128)(2,1)S(1)} %collective-permute-done.4), channel_id=1, source_target_pairs={{1,0},{2,1},{3,2},{4,3},{5,4},{6,5},{7,6},{9,8},{10,9},{11,10},{12... | collective-permute-start | bytes 196616 | tf_op jit(solution)/shard_map/while/body/eval_jaxpr/ppermute | solution.py:12
  298.5 41.1 %collective-permute-start.2 = (bf16[8,32,128]{2,1,0:T(8,128)(2,1)S(1)}, bf16[8,32,128]{2,1,0:T(8,128)(2,1)S(1)}, u32[]{:S(2)}, u32[]{:S(2)}) collective-permute-start(bf16[8,32,128]{2,1,0:T(8,128)(2,1)S(1)} %collective-permute-done.1), channel_id=1, source_target_pairs={{0,1},{1,2},{2,3},{3,4},{4,5},{5,6},{6,7},{8,9},{9,10},{10,11},{11... | collective-permute-start | bytes 196616 | tf_op jit(solution)/shard_map/while/body/eval_jaxpr/ppermute | solution.py:12
  331.5 10.0 %collective-permute-start.6 = (bf16[8,32,128]{2,1,0:T(8,128)(2,1)S(1)}, bf16[8,32,128]{2,1,0:T(8,128)(2,1)S(1)}, u32[]{:S(2)}, u32[]{:S(2)}) collective-permute-start(bf16[8,32,128]{2,1,0:T(8,128)(2,1)S(1)} %collective-permute-done.5), channel_id=1, source_target_pairs={{1,0},{2,1},{3,2},{4,3},{5,4},{6,5},{7,6},{9,8},{10,9},{11,10},{12... | collective-permute-start | bytes 196616 | tf_op jit(solution)/shard_map/while/body/eval_jaxpr/ppermute | solution.py:12
  341.5 5.6 collective-permute-start.7
  360.4 5.6 collective-permute-start.4
  362.8 5.1 collective-permute-start.1
  366.0 35.9 %collective-permute-start.5 = (bf16[8,32,128]{2,1,0:T(8,128)(2,1)S(1)}, bf16[8,32,128]{2,1,0:T(8,128)(2,1)S(1)}, u32[]{:S(2)}, u32[]{:S(2)}) collective-permute-start(bf16[8,32,128]{2,1,0:T(8,128)(2,1)S(1)} %collective-permute-done.4), channel_id=1, source_target_pairs={{1,0},{2,1},{3,2},{4,3},{5,4},{6,5},{7,6},{9,8},{10,9},{11,10},{12... | collective-permute-start | bytes 196616 | tf_op jit(solution)/shard_map/while/body/eval_jaxpr/ppermute | solution.py:12
  367.9 42.0 %collective-permute-start.2 = (bf16[8,32,128]{2,1,0:T(8,128)(2,1)S(1)}, bf16[8,32,128]{2,1,0:T(8,128)(2,1)S(1)}, u32[]{:S(2)}, u32[]{:S(2)}) collective-permute-start(bf16[8,32,128]{2,1,0:T(8,128)(2,1)S(1)} %collective-permute-done.1), channel_id=1, source_target_pairs={{0,1},{1,2},{2,3},{3,4},{4,5},{5,6},{6,7},{8,9},{9,10},{10,11},{11... | collective-permute-start | bytes 196616 | tf_op jit(solution)/shard_map/while/body/eval_jaxpr/ppermute | solution.py:12
  401.9 10.0 %collective-permute-start.6 = (bf16[8,32,128]{2,1,0:T(8,128)(2,1)S(1)}, bf16[8,32,128]{2,1,0:T(8,128)(2,1)S(1)}, u32[]{:S(2)}, u32[]{:S(2)}) collective-permute-start(bf16[8,32,128]{2,1,0:T(8,128)(2,1)S(1)} %collective-permute-done.5), channel_id=1, source_target_pairs={{1,0},{2,1},{3,2},{4,3},{5,4},{6,5},{7,6},{9,8},{10,9},{11,10},{12... | collective-permute-start | bytes 196616 | tf_op jit(solution)/shard_map/while/body/eval_jaxpr/ppermute | solution.py:12
  411.9 5.6 collective-permute-start.7
  430.8 5.6 collective-permute-start.4
  436.4 35.0 %collective-permute-start.5 = (bf16[8,32,128]{2,1,0:T(8,128)(2,1)S(1)}, bf16[8,32,128]{2,1,0:T(8,128)(2,1)S(1)}, u32[]{:S(2)}, u32[]{:S(2)}) collective-permute-start(bf16[8,32,128]{2,1,0:T(8,128)(2,1)S(1)} %collective-permute-done.4), channel_id=1, source_target_pairs={{1,0},{2,1},{3,2},{4,3},{5,4},{6,5},{7,6},{9,8},{10,9},{11,10},{12... | collective-permute-start | bytes 196616 | tf_op jit(solution)/shard_map/while/body/eval_jaxpr/ppermute | solution.py:12
  438.4 41.1 %collective-permute-start.2 = (bf16[8,32,128]{2,1,0:T(8,128)(2,1)S(1)}, bf16[8,32,128]{2,1,0:T(8,128)(2,1)S(1)}, u32[]{:S(2)}, u32[]{:S(2)}) collective-permute-start(bf16[8,32,128]{2,1,0:T(8,128)(2,1)S(1)} %collective-permute-done.1), channel_id=1, source_target_pairs={{0,1},{1,2},{2,3},{3,4},{4,5},{5,6},{6,7},{8,9},{9,10},{10,11},{11... | collective-permute-start | bytes 196616 | tf_op jit(solution)/shard_map/while/body/eval_jaxpr/ppermute | solution.py:12
  471.4 10.0 %collective-permute-start.6 = (bf16[8,32,128]{2,1,0:T(8,128)(2,1)S(1)}, bf16[8,32,128]{2,1,0:T(8,128)(2,1)S(1)}, u32[]{:S(2)}, u32[]{:S(2)}) collective-permute-start(bf16[8,32,128]{2,1,0:T(8,128)(2,1)S(1)} %collective-permute-done.5), channel_id=1, source_target_pairs={{1,0},{2,1},{3,2},{4,3},{5,4},{6,5},{7,6},{9,8},{10,9},{11,10},{12... | collective-permute-start | bytes 196616 | tf_op jit(solution)/shard_map/while/body/eval_jaxpr/ppermute | solution.py:12
  481.4 5.6 collective-permute-start.7
  500.3 5.6 collective-permute-start.4
  505.9 35.9 %collective-permute-start.5 = (bf16[8,32,128]{2,1,0:T(8,128)(2,1)S(1)}, bf16[8,32,128]{2,1,0:T(8,128)(2,1)S(1)}, u32[]{:S(2)}, u32[]{:S(2)}) collective-permute-start(bf16[8,32,128]{2,1,0:T(8,128)(2,1)S(1)} %collective-permute-done.4), channel_id=1, source_target_pairs={{1,0},{2,1},{3,2},{4,3},{5,4},{6,5},{7,6},{9,8},{10,9},{11,10},{12... | collective-permute-start | bytes 196616 | tf_op jit(solution)/shard_map/while/body/eval_jaxpr/ppermute | solution.py:12
  507.8 42.0 %collective-permute-start.2 = (bf16[8,32,128]{2,1,0:T(8,128)(2,1)S(1)}, bf16[8,32,128]{2,1,0:T(8,128)(2,1)S(1)}, u32[]{:S(2)}, u32[]{:S(2)}) collective-permute-start(bf16[8,32,128]{2,1,0:T(8,128)(2,1)S(1)} %collective-permute-done.1), channel_id=1, source_target_pairs={{0,1},{1,2},{2,3},{3,4},{4,5},{5,6},{6,7},{8,9},{9,10},{10,11},{11... | collective-permute-start | bytes 196616 | tf_op jit(solution)/shard_map/while/body/eval_jaxpr/ppermute | solution.py:12
  541.8 10.0 %collective-permute-start.6 = (bf16[8,32,128]{2,1,0:T(8,128)(2,1)S(1)}, bf16[8,32,128]{2,1,0:T(8,128)(2,1)S(1)}, u32[]{:S(2)}, u32[]{:S(2)}) collective-permute-start(bf16[8,32,128]{2,1,0:T(8,128)(2,1)S(1)} %collective-permute-done.5), channel_id=1, source_target_pairs={{1,0},{2,1},{3,2},{4,3},{5,4},{6,5},{7,6},{9,8},{10,9},{11,10},{12... | collective-permute-start | bytes 196616 | tf_op jit(solution)/shard_map/while/body/eval_jaxpr/ppermute | solution.py:12
  551.8 5.6 collective-permute-start.7
  (28 other events, 242.3 us)
where the time goes:
time: 572 us; the launch traced here: 569 us
  blocking collectives  225 us (39%)
  starting transfers between devices  207 us (36%)
  matrix products  48.9 us (9%)
  local copies, waits for them, and re-layouts  47.4 us (8%)
  waiting for transfers between devices  25.2 us (4%)
  other arithmetic  13.3 us (2%)
    ppermute x64, starting transfers between devices, shifted(): return lax.ppermute(value, axis, pairs)  207 us
    psum x8, blocking collectives, project(): summed = lax.psum(partial_value, 'blk')  178 us
    all_gather x8, blocking collectives, project(): result = lax.all_gather(summed[:, None], 'region', axis=1, tiled=True)  47.4 us
    dot_general x8, matrix products, advance(): jnp.einsum('bjpk,bjkm->bpm', gathered, near_tiles[0], preferred_element_t...  38.6 us
    ppermute x64, waiting for transfers between devices, shifted(): return lax.ppermute(value, axis, pairs)  25.2 us
    gather x8, local copies, waits for them, and re-layouts, advance(): gathered = history[delay_index, local_pos]  23.9 us
    slice x7, local copies, waits for them, and re-layouts, march(): history = jnp.concatenate([arrived[None], history[:-1]], axis=0)  12.7 us
    concatenate x7, other arithmetic, march(): history = jnp.concatenate([arrived[None], history[:-1]], axis=0)  11.5 us
  transfers between devices with their start and end apart: 64, of which 9 were waited for; matrix products, arithmetic and copies ran while one was open for 3% of the time, Pallas kernels for 0%

commit v1 on v0

v1 whole, which is shorter than its diff:
```python
import functools

import jax
import jax.numpy as jnp
from jax import lax
from jax.experimental import pallas as pl
from jax.experimental.pallas import tpu as pltpu
from jax.sharding import PartitionSpec as P

REACH = 4
CORES = 2
HOPS = (REACH + CORES - 1) // CORES
WIN = CORES * (2 * HOPS + 1)
F32 = jnp.float32
BF16 = jnp.bfloat16
MESH = pl.DeviceIdType.MESH


def march(
    regions, devices, chunks,
    cols_ref, delay_ref, slot_ref, pairs_ref, fdelay_ref,
    inc_hbm, past_hbm, sinv_hbm, tiles_hbm, fout_hbm, fin_hbm, cpl_hbm,
    out_ref,
    win, hist, tiles, inc, sinv, fout, fin, fin2, cpl, cpl2,
    msend, mrecv, msum, bsend, brecv, bl2, pos,
    in_sem, past_sem, tile_sem,
    own_send, fwd_send, own_recv, past_send, pastf_send, past_recv,
    m_send, m_recv, mp_send, mp_recv, b_send, b_recv,
):
    steps = inc_hbm.shape[0]
    dmax = past_hbm.shape[0]
    nb, near = tiles.shape[0], tiles.shape[1]
    per = nb // chunks
    pulses, rows = inc.shape[2], inc.shape[3]
    half, rank = pulses // 2, fout.shape[2]
    farp = cpl.shape[0]
    places = devices // CORES
    g = lax.axis_index("region")
    d = lax.axis_index("blk")
    z = d // CORES
    c = d % CORES
    mate = CORES * z + (1 - c)
    own = CORES * HOPS + c
    has_dn = d >= CORES
    has_up = d + CORES < devices

    past_in = [
        pltpu.make_async_copy(past_hbm.at[k, 0], win.at[dmax - 1 - k, own], past_sem.at[k])
        for k in range(dmax)
    ]
    small_in = [
        pltpu.make_async_copy(fout_hbm.at[0], fout, in_sem.at[0]),
        pltpu.make_async_copy(fin_hbm.at[0], fin, in_sem.at[1]),
        pltpu.make_async_copy(cpl_hbm.at[0], cpl, in_sem.at[2]),
        pltpu.make_async_copy(sinv_hbm.at[0], sinv, in_sem.at[3]),
        pltpu.make_async_copy(inc_hbm.at[:, 0], inc, in_sem.at[4]),
    ]
    tile_in = [
        pltpu.make_async_copy(tiles_hbm.at[0, b], tiles.at[b], tile_sem.at[b]) for b in range(nb)
    ]
    for copy in past_in + small_in + tile_in:
        copy.start()

    barrier = pltpu.get_barrier_semaphore()

    def greet(region, blk):
        pl.semaphore_signal(barrier, inc=1, device_id=(region, blk), device_id_type=MESH)

    greet(g, mate)

    @pl.when(has_dn)
    def _():
        greet(g, d - CORES)

    @pl.when(has_up)
    def _():
        greet(g, d + CORES)

    others = [(g + r) % regions for r in range(1, regions)]
    for g2 in others:
        for z2 in range(places):
            greet(g2, CORES * z2 + c)

    ends = has_dn.astype(jnp.int32) + has_up.astype(jnp.int32)
    pl.semaphore_wait(barrier, 1 + ends + (regions - 1) * places)

    def part(t, slot, ch, size):
        return win.at[t, slot, pl.ds(ch * size, size)]

    def send(t, ch, size, slot, slot2, dev, ssem, rsem):
        return pltpu.make_async_remote_copy(
            src_ref=part(t, slot, ch, size),
            dst_ref=part(t, slot2, ch, size),
            send_sem=ssem,
            recv_sem=rsem,
            device_id=(g, dev),
            device_id_type=MESH,
        )

    def own_copies(t, ch, size, ssem, rsem):
        return [
            (has_dn, send(t, ch, size, own, own + CORES, d - CORES, ssem.at[0], rsem.at[own + CORES])),
            (has_up, send(t, ch, size, own, own - CORES, d + CORES, ssem.at[1], rsem.at[own - CORES])),
            (None, send(t, ch, size, own, own, mate, ssem.at[2], rsem.at[own])),
        ]

    def arrivals(t, ch, size, hop, fsem, rsem):
        found = []
        for side, sign in enumerate((-1, 1)):
            source = d + sign * CORES * hop
            present = (source >= 0) & (source < devices)
            slot = own + sign * CORES * hop
            onward = d - sign * CORES
            more = present & (onward >= 0) & (onward < devices) if hop < HOPS else None
            forward = None
            if hop < HOPS:
                forward = send(
                    t, ch, size, slot, slot + sign * CORES, onward,
                    fsem.at[hop - 1, side, 0], rsem.at[slot + sign * CORES],
                )
            relay = send(t, ch, size, slot, slot, mate, fsem.at[hop - 1, side, 1], rsem.at[slot])
            found.append((present, slot, more, forward, relay))
        return found

    def guarded(cond, run):
        if cond is None:
            run()
        else:
            pl.when(cond)(run)

    def start(copies):
        for cond, copy in copies:
            guarded(cond, copy.start)

    def landed(t, ch, size, slot, rsem):
        ref = part(t, slot, ch, size)
        pltpu.make_async_copy(ref, ref, rsem.at[slot]).wait()

    def pass_on(t, ch, size, hop, fsem, rsem):
        for present, slot, more, forward, relay in arrivals(t, ch, size, hop, fsem, rsem):
            @pl.when(present)
            def _(slot=slot, relay=relay):
                landed(t, ch, size, slot, rsem)

            if forward is not None:
                pl.when(more)(forward.start)

            pl.when(present)(relay.start)

    def from_mate(t, ch, size, rsem):
        for hop in range(-HOPS, HOPS + 1):
            slot = CORES * HOPS + (1 - c) + CORES * hop
            source = mate + CORES * hop

            def take(slot=slot):
                landed(t, ch, size, slot, rsem)

            guarded(None if hop == 0 else (source >= 0) & (source < devices), take)

    def sent(t, ch, size, ssem, fsem, rsem):
        for cond, copy in own_copies(t, ch, size, ssem, rsem):
            guarded(cond, copy.wait_send)
        for hop in range(1, HOPS + 1):
            for present, slot, more, forward, relay in arrivals(t, ch, size, hop, fsem, rsem):
                if forward is not None:
                    pl.when(more)(forward.wait_send)
                pl.when(present)(relay.wait_send)

    def keep(t, ring):
        for k in range(WIN):
            source = CORES * (z - HOPS) + k

            @pl.when((source >= 0) & (source < devices))
            def _(k=k):
                hist[pl.ds((ring * WIN + k) * nb, nb)] = win[t, k]

    def pack(moment):
        return jnp.concatenate([moment[:half], moment[half:]], axis=1)

    def moment_copies(t, source, ssem, rsem):
        copies = []
        for r, g2 in enumerate(others):
            for z2 in range(places):
                copies.append(
                    pltpu.make_async_remote_copy(
                        src_ref=source,
                        dst_ref=mrecv.at[t, g, z],
                        send_sem=ssem.at[r, z2],
                        recv_sem=rsem.at[g, z],
                        device_id=(g2, CORES * z2 + c),
                        device_id_type=MESH,
                    )
                )
        return copies

    def take_moments(t, ring, rsem):
        for g2 in others:
            total = None
            for z2 in range(places):
                ref = mrecv.at[t, g2, z2]
                pltpu.make_async_copy(ref, ref, rsem.at[g2, z2]).wait()
            for z2 in range(places):
                value = mrecv[t, g2, z2].astype(F32)
                total = value if total is None else total + value
            msum[ring, g2] = total

    def blend(n, parity):
        total = None
        for p in range(farp):
            ring = lax.rem(n + dmax - fdelay_ref[0, p], dmax)
            value = jnp.dot(
                msum[ring, pairs_ref[0, p]], cpl2[p],
                preferred_element_type=F32, precision=lax.Precision.HIGHEST,
            )
            total = value if total is None else total + value
        bsend[...] = total
        copy = pltpu.make_async_remote_copy(
            src_ref=bsend, dst_ref=brecv.at[parity], send_sem=b_send, recv_sem=b_recv.at[parity],
            device_id=(g, mate), device_id_type=MESH,
        )
        copy.start()
        copy.wait()
        both = (total + brecv[parity]).astype(BF16)
        lane = lax.broadcasted_iota(jnp.int32, both.shape, 1)
        zero = jnp.zeros_like(both)
        bl2[...] = jnp.concatenate(
            [jnp.where(lane < rank, both, zero), jnp.where(lane < rank, zero, both)], axis=0
        )

    for k in range(dmax):
        past_in[k].wait()
    for t in range(dmax):
        start(own_copies(t, 0, nb, past_send.at[t], past_recv.at[t]))
    small_in[0].wait()
    for t in range(dmax):
        moment = None
        for b in range(nb):
            value = jnp.dot(win[t, own, b], fout[b], preferred_element_type=F32)
            moment = value if moment is None else moment + value
        msend[t] = pack(moment).astype(BF16)
    for t in range(dmax):
        for copy in moment_copies(t, msend.at[t], mp_send.at[t], mp_recv.at[t]):
            copy.start()

    def place(i, carry):
        b, j = i // near, i % near
        where = slot_ref[0, cols_ref[0, b, j]] - CORES * (z - HOPS) * nb
        pos[i] = jnp.minimum(jnp.maximum(where, 0), WIN * nb - 1)
        return carry

    lax.fori_loop(0, nb * near, place, 0)
    small_in[1].wait()
    small_in[2].wait()
    for b in range(nb):
        fin2[b, :rank] = fin[b]
        fin2[b, rank:] = fin[b]
    for p in range(farp):
        value = cpl[p]
        blank = jnp.zeros_like(value)
        cpl2[p, :rank] = jnp.concatenate([value, blank], axis=1)
        cpl2[p, rank:] = jnp.concatenate([blank, value], axis=1)

    for hop in range(1, HOPS + 1):
        for t in range(dmax):
            pass_on(t, 0, nb, hop, pastf_send.at[t], past_recv.at[t])
    for t in range(dmax):
        take_moments(t, t, mp_recv.at[t])
    blend(0, 0)
    for t in range(dmax):
        from_mate(t, 0, nb, past_recv.at[t])
        keep(t, t)
    for t in range(dmax):
        sent(t, 0, nb, past_send.at[t], pastf_send.at[t], past_recv.at[t])
        for copy in moment_copies(t, msend.at[t], mp_send.at[t], mp_recv.at[t]):
            copy.wait_send()
    small_in[3].wait()
    small_in[4].wait()
    for copy in tile_in:
        copy.wait()

    def current_of(n, b):
        pieces = []
        for j in range(near):
            ring = lax.rem(n + dmax - delay_ref[0, b, j], dmax)
            pieces.append(hist[ring * (WIN * nb) + pos[b * near + j]])
        gathered = jnp.concatenate(pieces, axis=1)
        field = jnp.dot(gathered, tiles[b].reshape(near * rows, rows), preferred_element_type=F32)
        far = jnp.dot(bl2[...], fin2[b], preferred_element_type=F32)
        driven = (inc[n, b].astype(F32) - field - far).astype(BF16)
        return jnp.dot(driven, sinv[b], preferred_element_type=F32).astype(BF16)

    def step(n, carry):
        t = n + dmax
        parity = n % 2
        later = (n + 1) % 2

        def sems(ch):
            return own_send.at[ch], fwd_send.at[ch], own_recv.at[parity, ch]

        def chunk(ch, moment):
            for i in range(per):
                b = ch * per + i
                value = current_of(n, b)
                win[t, own, b] = value
                out_ref[n, 0, b] = value
                moment = moment + jnp.dot(value, fout[b], preferred_element_type=F32)
            ssem, fsem, rsem = sems(ch)
            start(own_copies(t, ch, per, ssem, rsem))
            return moment

        moment = lax.fori_loop(0, chunks, chunk, jnp.zeros((pulses, rank), F32))
        msend[0] = pack(moment).astype(BF16)
        far_copies = moment_copies(t, msend.at[0], m_send, m_recv.at[parity])
        for copy in far_copies:
            copy.start()
        for hop in range(1, HOPS + 1):
            for ch in range(chunks):
                ssem, fsem, rsem = sems(ch)
                pass_on(t, ch, per, hop, fsem, rsem)
        ring = lax.rem(t, dmax)
        take_moments(t, ring, m_recv.at[parity])
        blend(n + 1, later)
        for ch in range(chunks):
            ssem, fsem, rsem = sems(ch)
            from_mate(t, ch, per, rsem)
        keep(t, ring)
        for ch in range(chunks):
            ssem, fsem, rsem = sems(ch)
            sent(t, ch, per, ssem, fsem, rsem)
        for copy in far_copies:
            copy.wait_send()
        return carry

    lax.fori_loop(0, steps - 1, step, 0)

    def last(b, carry):
        out_ref[steps - 1, 0, b] = current_of(steps - 1, b)
        return carry

    lax.fori_loop(0, nb, last, 0)


def on_device(
    regions, devices,
    incident, past_currents, self_inverse, near_tiles, near_cols, near_delay,
    block_slot, far_out, far_in, far_pairs, far_delay, far_coupling,
):
    steps, _, nb, pulses, rows = incident.shape
    dmax = past_currents.shape[0]
    near = near_cols.shape[2]
    rank = far_out.shape[3]
    farp = far_pairs.shape[1]
    places = devices // CORES
    half = pulses // 2
    chunks = 4
    times = dmax + steps - 1
    dma = pltpu.SemaphoreType.DMA
    smem = pl.BlockSpec(memory_space=pltpu.SMEM)
    anywhere = pl.BlockSpec(memory_space=pl.ANY)
    scratch = [
        pltpu.VMEM((times, WIN, nb, pulses, rows), BF16),
        pltpu.VMEM((dmax * WIN * nb, pulses, rows), BF16),
        pltpu.VMEM((nb, near, rows, rows), BF16),
        pltpu.VMEM((steps, nb, pulses, rows), BF16),
        pltpu.VMEM((nb, rows, rows), BF16),
        pltpu.VMEM((nb, rows, rank), BF16),
        pltpu.VMEM((nb, rank, rows), BF16),
        pltpu.VMEM((nb, 2 * rank, rows), BF16),
        pltpu.VMEM((farp, rank, rank), F32),
        pltpu.VMEM((farp, 2 * rank, 2 * rank), F32),
        pltpu.VMEM((dmax, half, 2 * rank), BF16),
        pltpu.VMEM((times, regions, places, half, 2 * rank), BF16),
        pltpu.VMEM((dmax, regions, half, 2 * rank), F32),
        pltpu.VMEM((half, 2 * rank), F32),
        pltpu.VMEM((2, half, 2 * rank), F32),
        pltpu.VMEM((pulses, 2 * rank), BF16),
        pltpu.SMEM((nb * near,), jnp.int32),
        dma((5,)),
        dma((dmax,)),
        dma((nb,)),
        dma((chunks, 3)),
        dma((chunks, HOPS, 2, 2)),
        dma((2, chunks, WIN)),
        dma((dmax, 3)),
        dma((dmax, HOPS, 2, 2)),
        dma((dmax, WIN)),
        dma((regions - 1, places)),
        dma((2, regions, places)),
        dma((dmax, regions - 1, places)),
        dma((dmax, regions, places)),
        dma,
        dma((2,)),
    ]
    return pl.pallas_call(
        functools.partial(march, regions, devices, chunks),
        out_shape=jax.ShapeDtypeStruct(incident.shape, BF16),
        in_specs=[smem] * 5 + [anywhere] * 7,
        out_specs=pl.BlockSpec(memory_space=pltpu.VMEM),
        scratch_shapes=scratch,
        compiler_params=pltpu.CompilerParams(
            collective_id=0, has_side_effects=True, vmem_limit_bytes=56 * 1024 * 1024
        ),
        name="march",
    )(
        near_cols, near_delay, block_slot, far_pairs, far_delay,
        incident, past_currents, self_inverse, near_tiles, far_out, far_in, far_coupling,
    )


def solution(mesh):
    in_specs = (
        P(None, "region", "blk", None, None),
        P(None, "region", "blk", None, None),
        P("region", "blk", None, None),
        P("region", "blk", None, None, None),
        P("region", "blk", None),
        P("region", "blk", None),
        P("region", None),
        P("region", "blk", None, None),
        P("region", "blk", None, None),
        P("region", None),
        P("region", None),
        P("region", None, None, None),
    )
    out_specs = P(None, "region", "blk", None, None)
    body = functools.partial(on_device, mesh.shape["region"], mesh.shape["blk"])
    return jax.shard_map(
        body, mesh=mesh, in_specs=in_specs, out_specs=out_specs, check_vma=False
    )
```

time: 572 us -> 112 us (0.20)
  blocking collectives: 225 us -> 0 us
  starting transfers between devices: 207 us -> 0 us
  Pallas kernels: 0 us -> 108 us
  matrix products: 48.9 us -> 0 us
  local copies, waits for them, and re-layouts: 47.4 us -> 3.61 us
  waiting for transfers between devices: 25.2 us -> 0 us
  other arithmetic: 13.3 us -> 0 us
    ppermute x64 -> x0, starting transfers between devices: 207 us -> none  [shifted(): return lax.ppermute(value, axis, pairs)]
    psum x8 -> x0, blocking collectives: 178 us -> none  [project(): summed = lax.psum(partial_value, 'blk')]
    pallas_call x0 -> x1, Pallas kernels: none -> 108 us  [on_device(): pl.pallas_call(functools.partial(march, regions, devices, chunks), out_sh...]
    dot_general x32 -> x0, matrix products: 48.9 us -> none  [the longest x8 38.6 us: advance(): jnp.einsum('bjpk,bjkm->bpm', gathered, near_tiles[0], preferred_element_t...]
    all_gather x8 -> x0, blocking collectives: 47.4 us -> none  [project(): result = lax.all_gather(summed[:, None], 'region', axis=1, tiled=True)]
    gather x17 -> x0, local copies, waits for them, and re-layouts: 30.3 us -> none  [the longest x8 23.9 us: advance(): gathered = history[delay_index, local_pos]]
    ppermute x64 -> x0, waiting for transfers between devices: 25.2 us -> none  [shifted(): return lax.ppermute(value, axis, pairs)]
    slice x14 -> x0, local copies, waits for them, and re-layouts: 12.8 us -> none  [the longest x7 12.7 us: march(): history = jnp.concatenate([arrived[None], history[:-1]], axis=0)]
  transfers between devices with their start and end apart: 64 -> 0, of which waited for: 9 -> 0; matrix products, arithmetic and copies ran while one was open for 3% -> 0% of each run, Pallas kernels for 0% -> 0%
where the time goes in v1:
time: 112 us; the launch traced here: 111 us
  Pallas kernels  108 us (96%)
  local copies, waits for them, and re-layouts  3.61 us (3%)
    pallas_call x1, Pallas kernels, on_device(): pl.pallas_call(functools.partial(march, regions, devices, chunks), out_sh...  108 us
    unnamed x2, local copies, waits for them, and re-layouts  3.61 us

profile of v1, /device:TPU:1, one launch (start us, length us, event | category | flops | bytes accessed | tf_op | source)
XLA Modules:
  0.0 111.4 jit_solution(9220410273382716624)
XLA Ops:
  0.0 1.7 %copy.13.fout_hbm = bf16[1,8,128,64]{3,2,1,0:T(8,128)(2,1)} copy(bf16[1,8,128,64]{2,3,1,0:T(8,128)(2,1)} %param.19) | data formatting | bytes 262144 | tf_op args[7]
  1.7 107.8 %march.1 = bf16[8,1,8,32,128]{4,3,2,1,0:T(8,128)(2,1)} custom-call(s32[1,8,32]{2,1,0:T(8,128)} %cols_ref.1, s32[1,8,32]{2,1,0:T(8,128)} %delay_ref.1, s32[1,64]{1,0:T(1,128)} %slot_ref.1, s32[1,3]{1,0:T(1,128)} %pairs_ref.1, s32[1,3]{1,0:T(1,128)} %fdelay_ref.1, bf16[8,1,8,32,128]{4,3,2,1,0:T(8,128)(2,1)} %inc_hbm.1, bf16[4,1,8,32,128]{4,3,2,1,0:T(8,128)(2,1)} %past_hbm.1, ...), custom_call_target="tpu_custom_call" | custom-call | tf_op jit(solution)/shard_map/march/pallas_call | solution.py:394
  109.5 1.9 %copy.15 = bf16[8,1,8,32,128]{4,3,2,1,0:T(8,128)(2,1)} copy(bf16[8,1,8,32,128]{4,3,2,1,0:T(8,128)(2,1)} %march.1) | data formatting | bytes 1048576
